TPU v7x, 128 devices: a whole 4x4x4 slice. The times are simulated.
128 devices in a mesh: seq: 32 (over z, x, core), group: 4 (over y).
Axes of the slice: x: 4, y: 4, z: 4, core: 2. Of those that a mesh axis runs over, the one named last changes fastest.
Arguments:
- new_queries: bfloat16 [32, 8, 8, 128], P('seq', 'group'), may hold values from -6 to 6
- stored_keys: bfloat16 [32, 8, 16384, 128], P(None, 'group', 'seq'), may hold values from -6 to 6
- stored_values: bfloat16 [32, 8, 16384, 128], P(None, 'group', 'seq'), may hold values from -6 to 6
- used_length: int32 [32], replicated, may hold values from 8192 to 16384
- out_weight: bfloat16 [8, 8, 128, 5120], P('group'), may hold values from -0.0625 to 0.0625
Outputs:
- token_out: bfloat16 [32, 5120], P('seq', 'group')
All inputs are finite; a program needn't handle non-finite values.
Results may differ from a plain program's by a relative error of at most 0.0025.
Values may be sent and summed in bfloat16 or wider, within the bound.
No kernel may reach another device: no remote copies, remote signals or barrier semaphores. Data moves between devices by JAX's collectives and lax.ppermute only.
A program may use at most 128 MiB of HBM per device.

v0:
```python
import jax
import jax.numpy as jnp
from jax import lax
from jax.sharding import PartitionSpec as P

HEAD_SIZE = 128


def per_device(new_queries, stored_keys, stored_values, used_length, out_weight):
    all_queries = lax.all_gather(new_queries, "seq", axis=0, tiled=True)
    logit = jnp.einsum(
        "bkgd,bktd->bkgt", all_queries, stored_keys, preferred_element_type=jnp.float32
    ) * HEAD_SIZE ** (-0.5)
    positions = lax.axis_index("seq") * stored_keys.shape[2] + jnp.arange(stored_keys.shape[2])
    filled = positions[None, :] < used_length[:, None]
    logit = jnp.where(filled[:, None, None, :], logit, -1e30)
    top = jnp.max(logit, axis=-1)
    part = jnp.where(filled[:, None, None, :], jnp.exp(logit - top[..., None]), 0.0)
    weight_sum = jnp.sum(part, axis=-1)
    read_sum = jnp.einsum(
        "bkgt,bktd->bkgd", part, stored_values.astype(jnp.float32), precision=lax.Precision.HIGHEST
    )
    tops, sums, parts = (
        lax.all_to_all(top[None], "seq", split_axis=1, concat_axis=0, tiled=True),
        lax.all_to_all(weight_sum[None], "seq", split_axis=1, concat_axis=0, tiled=True),
        lax.all_to_all(read_sum[None], "seq", split_axis=1, concat_axis=0, tiled=True),
    )
    best = jnp.max(tops, axis=0)
    scale = jnp.exp(tops - best)
    weight_own = jnp.sum(sums * scale, axis=0)
    read_own = jnp.sum(parts * scale[..., None], axis=0)
    read = (read_own / weight_own[..., None]).astype(jnp.bfloat16)
    term = jnp.einsum("bkgd,kgdm->bm", read, out_weight, preferred_element_type=jnp.float32)
    token_out = lax.psum_scatter(term, "group", scatter_dimension=1, tiled=True).astype(
        jnp.bfloat16
    )
    return token_out


def solution(mesh):
    in_specs = (
        P("seq", "group", None, None),
        P(None, "group", "seq", None),
        P(None, "group", "seq", None),
        P(),
        P("group", None, None, None),
    )
    out_specs = P("seq", "group")
    return jax.shard_map(
        per_device, mesh=mesh, in_specs=in_specs, out_specs=out_specs, check_vma=False
    )
```

profile of v0, /device:TPU:1, one launch (start us, length us, event | category | flops | bytes accessed | tf_op | source)
XLA Modules:
  0.0 134.0 jit_solution(4825849419178507323)
XLA Ops:
  6.5 27.3 %all_gather.3 = bf16[32,2,8,128]{3,2,1,0:T(8,128)(2,1)S(1)} all-gather(bf16[1,2,8,128]{3,2,1,0:T(8,128)(2,1)} %param.5), channel_id=1, replica_groups=mesh['seq'=32,'group'=4] {'seq'}, dimensions={0}, use_global_device_ids=true | all-gather | bytes 135168 | tf_op jit(solution)/shard_map/all_gather | solution.py:10
  33.9 0.7 broadcast_compare_fusion
  34.6 6.4 %fusion.18 = (f32[32,2,8]{2,1,0:T(2,128)}, f32[32,2,8,512]{3,2,1,0:T(8,128)S(1)}) fusion(bf16[32,2,8,128]{3,2,1,0:T(8,128)(2,1)S(1)} %all_gather.3, bf16[32,2,512,128]{3,2,1,0:T(8,128)(2,1)} %param.6, pred[32,512]{1,0:T(8,128)(4,1)S(1)} %broadcast_compare_fusion), kind=kOutput, calls=%fused_computation.25 | convolution fusion | flops 67894784 | bytes 9586688 | tf_op jit(solution)/shard_map/bkgd,bktd->bkgt/dot_general | solution.py:11
  41.0 4.9 %all-to-all-start.1 = ((f32[1,32,2,8]{3,2,0,1:T(2,128)}), f32[1,32,2,8]{3,2,0,1:T(2,128)S(1)}, u32[]{:S(2)}, u32[]{:S(2)}) async-start(f32[1,32,2,8]{3,2,0,1:T(2,128)} %bitcast.3), calls=%async_computation.1 | async-start | bytes 65536 | tf_op jit(solution)/shard_map/all_to_all | solution.py:24
  45.9 1.8 %fusion.6 = f32[32,2,8]{2,1,0:T(2,128)} fusion(f32[32,2,8,512]{3,2,1,0:T(8,128)S(1)} %get-tuple-element.6, f32[32,2,8]{2,1,0:T(2,128)} %get-tuple-element.5, pred[32,512]{1,0:T(8,128)(4,1)S(1)} %broadcast_compare_fusion), kind=kLoop, calls=%fused_computation.7 | loop fusion | flops 785920 | bytes 1069056 | tf_op jit(solution)/shard_map/reduce_sum | solution.py:19
  47.6 5.5 %all-to-all-done.1 = f32[1,32,2,8]{3,2,0,1:T(2,128)S(1)} async-done(((f32[1,32,2,8]{3,2,0,1:T(2,128)}), f32[1,32,2,8]{3,2,0,1:T(2,128)S(1)}, u32[]{:S(2)}, u32[]{:S(2)}) %all-to-all-start.1) | async-done | bytes 2080 | tf_op jit(solution)/shard_map/all_to_all | solution.py:24
  53.1 3.9 %all-to-all-start.2 = ((f32[1,32,2,8]{3,2,0,1:T(2,128)}), f32[1,32,2,8]{3,2,0,1:T(2,128)S(1)}, u32[]{:S(2)}, u32[]{:S(2)}) async-start(f32[1,32,2,8]{3,2,0,1:T(2,128)} %bitcast.5), calls=%async_computation.2 | async-start | bytes 65536 | tf_op jit(solution)/shard_map/all_to_all | solution.py:25
  57.0 6.5 %convolution_bitcast_fusion = f32[1,32,2,8,128]{4,3,2,0,1:T(8,128)} fusion(bf16[32,2,512,128]{3,2,1,0:T(8,128)(2,1)} %param.7, f32[32,2,8,512]{3,2,1,0:T(8,128)S(1)} %get-tuple-element.6, f32[32,2,8]{2,1,0:T(2,128)} %get-tuple-element.5, pred[32,512]{1,0:T(8,128)(4,1)S(1)} %broadcast_compare_fusion), kind=kOutput, calls=%fused_computation.5 | convolution fusion | flops 403177472 | bytes 9717760 | tf_op jit(solution)/shard_map/bkgt,bktd->bkgd/dot_general | solution.py:20
  63.6 0.8 all-to-all-done.2
  64.4 6.7 %all-to-all-start = ((f32[1,32,2,8,128]{4,3,2,0,1:T(8,128)}), f32[1,32,2,8,128]{4,3,2,0,1:T(8,128)S(1)}, u32[]{:S(2)}, u32[]{:S(2)}) async-start(f32[1,32,2,8,128]{4,3,2,0,1:T(8,128)} %convolution_bitcast_fusion), calls=%async_computation | async-start | bytes 524288 | tf_op jit(solution)/shard_map/all_to_all | solution.py:26
  71.1 0.0 reduce-scatter.4.cloned.1.call-start
  71.1 0.1 fusion.14
  71.2 8.7 %all-to-all-done = f32[1,32,2,8,128]{4,3,2,0,1:T(8,128)S(1)} async-done(((f32[1,32,2,8,128]{4,3,2,0,1:T(8,128)}), f32[1,32,2,8,128]{4,3,2,0,1:T(8,128)S(1)}, u32[]{:S(2)}, u32[]{:S(2)}) %all-to-all-start) | async-done | bytes 262176 | tf_op jit(solution)/shard_map/all_to_all | solution.py:26
  80.0 0.1 fusion.10
  80.1 0.1 fusion.16
  80.2 13.4 %fusion.2 = f32[5120,1]{1,0:T(8,128)} fusion(bf16[2,8,128,5120]{3,2,1,0:T(8,128)(2,1)} %param.9, bf16[2,8,128,1]{2,1,0,3:T(8,128)(2,1)S(1)} %fusion.16), kind=kOutput, calls=%fused_computation.2 | convolution fusion | flops 20971520 | bytes 20996096 | tf_op jit(solution)/shard_map/bkgd,kgdm->bm/dot_general | solution.py:33
  93.6 0.0 reduce-scatter.4.cloned.1.call-update
  93.6 31.6 %reduce-scatter.4.cloned.1.call-done = f32[1280,1]{1,0:T(8,128)} async-done(((f32[5120,1]{1,0:T(8,128)}), f32[1280,1]{1,0:T(8,128)}) %reduce-scatter.4.cloned.1.call-update) | async-done | bytes 5136
  125.3 1.9 %copy.11 = bf16[1,1280]{1,0:T(2,128)(2,1)} copy(f32[1,1280]{0,1:T(8,128)} %bitcast.41) | data formatting | bytes 7680
  (3 shorter events, 0.1 us)
Async XLA Ops:
  41.0 12.2 %all-to-all-start.1 = ((f32[1,32,2,8]{3,2,0,1:T(2,128)}), f32[1,32,2,8]{3,2,0,1:T(2,128)S(1)}, u32[]{:S(2)}, u32[]{:S(2)}) async-start(f32[1,32,2,8]{3,2,0,1:T(2,128)} %bitcast.3), calls=%async_computation.1 | async-start | bytes 65536 | tf_op jit(solution)/shard_map/all_to_all | solution.py:24
  53.1 11.3 %all-to-all-start.2 = ((f32[1,32,2,8]{3,2,0,1:T(2,128)}), f32[1,32,2,8]{3,2,0,1:T(2,128)S(1)}, u32[]{:S(2)}, u32[]{:S(2)}) async-start(f32[1,32,2,8]{3,2,0,1:T(2,128)} %bitcast.5), calls=%async_computation.2 | async-start | bytes 65536 | tf_op jit(solution)/shard_map/all_to_all | solution.py:25
  64.4 15.6 %all-to-all-start = ((f32[1,32,2,8,128]{4,3,2,0,1:T(8,128)}), f32[1,32,2,8,128]{4,3,2,0,1:T(8,128)S(1)}, u32[]{:S(2)}, u32[]{:S(2)}) async-start(f32[1,32,2,8,128]{4,3,2,0,1:T(8,128)} %convolution_bitcast_fusion), calls=%async_computation | async-start | bytes 524288 | tf_op jit(solution)/shard_map/all_to_all | solution.py:26
  71.1 54.2 %reduce-scatter.4.cloned.1.call-start = ((), (), s32[]{:S(2)}) async-start(), calls=%async_computation.4 | async-start | bytes 3276800
Sparse Core Ops, SparseCore 0:
  93.8 31.4 reduce-scatter.3
where the time goes:
time: 135 us; the launch traced here: 134 us
  waiting for transfers between devices  46.7 us (35%)
  blocking collectives  27.3 us (20%)
  matrix products  26.3 us (19%)
  starting transfers between devices  15.5 us (11%)
  between operations  13.4 us (10%)
  other arithmetic  2.83 us (2%)
  local copies, waits for them, and re-layouts  1.91 us (1%)
    unnamed x2, waiting for transfers between devices  31.6 us
    all_gather x1, blocking collectives, per_device(): all_queries = lax.all_gather(new_queries, 'seq', axis=0, tiled=True)  27.3 us
    dot_general x1, matrix products, per_device(): jnp.einsum('bkgd,kgdm->bm', read, out_weight, preferred_element_type=jnp....  13.4 us
    all_to_all x1, waiting for transfers between devices, per_device(): lax.all_to_all(read_sum[None], 'seq', split_axis=1, concat_axis=0, tiled=...  8.74 us
    all_to_all x1, starting transfers between devices, per_device(): lax.all_to_all(read_sum[None], 'seq', split_axis=1, concat_axis=0, tiled=...  6.68 us
    dot_general x1, matrix products, per_device(): jnp.einsum('bkgt,bktd->bkgd', part, stored_values.astype(jnp.float32), pr...  6.5 us
    dot_general x1, matrix products, per_device(): jnp.einsum('bkgd,bktd->bkgt', all_queries, stored_keys, preferred_element...  6.36 us
    all_to_all x1, waiting for transfers between devices, per_device(): lax.all_to_all(top[None], 'seq', split_axis=1, concat_axis=0, tiled=True)  5.49 us
  transfers between devices with their start and end apart: 4, of which 4 were waited for; matrix products, arithmetic and copies ran while one was open for 6% of the time, Pallas kernels for 0%

commit v1 on v0

--- a/solution.py
+++ b/solution.py
@@ -7,7 +7,10 @@
 
 
 def per_device(new_queries, stored_keys, stored_values, used_length, out_weight):
-    all_queries = lax.all_gather(new_queries, "seq", axis=0, tiled=True)
+    n_dev = lax.axis_size("seq")
+    tiles = jnp.stack([new_queries for _ in range(n_dev)])
+    tiles = lax.all_to_all(tiles, "seq", split_axis=0, concat_axis=0)
+    all_queries = jnp.concatenate(tiles, axis=0)
     logit = jnp.einsum(
         "bkgd,bktd->bkgt", all_queries, stored_keys, preferred_element_type=jnp.float32
     ) * HEAD_SIZE ** (-0.5)

time: 135 us -> 124 us (0.919)
  blocking collectives: 27.3 us -> 0 us
  starting transfers between devices: 15.5 us -> 23.9 us
  waiting for transfers between devices: 46.7 us -> 53.7 us
    all_gather x1 -> x0, blocking collectives: 27.3 us -> none  [per_device(): all_queries = lax.all_gather(new_queries, 'seq', axis=0, tiled=True)]
    all_to_all x0 -> x1, starting transfers between devices: none -> 9.42 us  [per_device(): tiles = lax.all_to_all(tiles, 'seq', split_axis=0, concat_axis=0)]
    all_to_all x0 -> x1, waiting for transfers between devices: none -> 6.84 us  [per_device(): tiles = lax.all_to_all(tiles, 'seq', split_axis=0, concat_axis=0)]
  transfers between devices with their start and end apart: 4 -> 5, of which waited for: 4 -> 5; matrix products, arithmetic and copies ran while one was open for 6% -> 7% of each run, Pallas kernels for 0% -> 0%
where the time goes in v1:
time: 124 us; the launch traced here: 123 us
  waiting for transfers between devices  53.7 us (43%)
  matrix products  26.3 us (21%)
  starting transfers between devices  23.9 us (19%)
  between operations  13.5 us (11%)
  local copies, waits for them, and re-layouts  3.25 us (3%)
  other arithmetic  2.84 us (2%)
    unnamed x2, waiting for transfers between devices  31.6 us
    dot_general x1, matrix products, per_device(): jnp.einsum('bkgd,kgdm->bm', read, out_weight, preferred_element_type=jnp....  13.4 us
    all_to_all x1, starting transfers between devices, per_device(): tiles = lax.all_to_all(tiles, 'seq', split_axis=0, concat_axis=0)  9.42 us
    all_to_all x1, waiting for transfers between devices, per_device(): lax.all_to_all(read_sum[None], 'seq', split_axis=1, concat_axis=0, tiled=...  8.74 us
    all_to_all x1, waiting for transfers between devices, per_device(): tiles = lax.all_to_all(tiles, 'seq', split_axis=0, concat_axis=0)  6.84 us
    all_to_all x1, starting transfers between devices, per_device(): lax.all_to_all(read_sum[None], 'seq', split_axis=1, concat_axis=0, tiled=...  6.69 us
    dot_general x1, matrix products, per_device(): jnp.einsum('bkgt,bktd->bkgd', part, stored_values.astype(jnp.float32), pr...  6.5 us
    dot_general x1, matrix products, per_device(): jnp.einsum('bkgd,bktd->bkgt', all_queries, stored_keys, preferred_element...  6.36 us
  transfers between devices with their start and end apart: 5, of which 5 were waited for; matrix products, arithmetic and copies ran while one was open for 7% of the time, Pallas kernels for 0%

profile of v1, /device:TPU:1, one launch (start us, length us, event | category | flops | bytes accessed | tf_op | source)
XLA Modules:
  0.0 123.4 jit_solution(12774483349527996605)
XLA Ops:
  6.5 1.3 %stack.2 = bf16[32,1,2,8,128]{4,3,2,1,0:T(8,128)(2,1)} broadcast(bf16[2,8,128]{2,1,0:T(8,128)(2,1)} %bitcast.47), dimensions={2,3,4} | broadcast | bytes 135168 | tf_op jit(solution)/shard_map/stack | solution.py:11
  7.9 9.4 %all-to-all-start = ((bf16[32,1,2,8,128]{4,3,2,1,0:T(8,128)(2,1)}), bf16[32,1,2,8,128]{4,3,2,1,0:T(8,128)(2,1)S(1)}, u32[]{:S(2)}, u32[]{:S(2)}) async-start(bf16[32,1,2,8,128]{4,3,2,1,0:T(8,128)(2,1)} %stack.2), calls=%async_computation | async-start | bytes 262144 | tf_op jit(solution)/shard_map/all_to_all | solution.py:12
  17.3 0.7 broadcast_compare_fusion
  18.1 6.8 %all-to-all-done = bf16[32,1,2,8,128]{4,3,2,1,0:T(8,128)(2,1)S(1)} async-done(((bf16[32,1,2,8,128]{4,3,2,1,0:T(8,128)(2,1)}), bf16[32,1,2,8,128]{4,3,2,1,0:T(8,128)(2,1)S(1)}, u32[]{:S(2)}, u32[]{:S(2)}) %all-to-all-start) | async-done | bytes 131104 | tf_op jit(solution)/shard_map/all_to_all | solution.py:12
  24.9 6.4 %fusion.19 = (f32[32,2,8]{2,1,0:T(2,128)}, f32[32,2,8,512]{3,2,1,0:T(8,128)S(1)}) fusion(bf16[32,2,512,128]{3,2,1,0:T(8,128)(2,1)} %param.6, bf16[32,1,2,8,128]{4,3,2,1,0:T(8,128)(2,1)S(1)} %all-to-all-done, pred[32,512]{1,0:T(8,128)(4,1)S(1)} %broadcast_compare_fusion), kind=kOutput, calls=%fused_computation.26 | convolution fusion | flops 67894784 | bytes 9586688 | tf_op jit(solution)/shard_map/bkgd,bktd->bkgt/dot_general | solution.py:14
  31.3 3.9 %all-to-all-start.2 = ((f32[1,32,2,8]{3,2,0,1:T(2,128)}), f32[1,32,2,8]{3,2,0,1:T(2,128)S(1)}, u32[]{:S(2)}, u32[]{:S(2)}) async-start(f32[1,32,2,8]{3,2,0,1:T(2,128)} %bitcast.5), calls=%async_computation.2 | async-start | bytes 65536 | tf_op jit(solution)/shard_map/all_to_all | solution.py:27
  35.2 1.8 %fusion.6 = f32[32,2,8]{2,1,0:T(2,128)} fusion(f32[32,2,8,512]{3,2,1,0:T(8,128)S(1)} %get-tuple-element.6, f32[32,2,8]{2,1,0:T(2,128)} %get-tuple-element.5, pred[32,512]{1,0:T(8,128)(4,1)S(1)} %broadcast_compare_fusion), kind=kLoop, calls=%fused_computation.7 | loop fusion | flops 785920 | bytes 1069056 | tf_op jit(solution)/shard_map/reduce_sum | solution.py:22
  36.9 5.6 %all-to-all-done.2 = f32[1,32,2,8]{3,2,0,1:T(2,128)S(1)} async-done(((f32[1,32,2,8]{3,2,0,1:T(2,128)}), f32[1,32,2,8]{3,2,0,1:T(2,128)S(1)}, u32[]{:S(2)}, u32[]{:S(2)}) %all-to-all-start.2) | async-done | bytes 2080 | tf_op jit(solution)/shard_map/all_to_all | solution.py:27
  42.5 3.9 %all-to-all-start.3 = ((f32[1,32,2,8]{3,2,0,1:T(2,128)}), f32[1,32,2,8]{3,2,0,1:T(2,128)S(1)}, u32[]{:S(2)}, u32[]{:S(2)}) async-start(f32[1,32,2,8]{3,2,0,1:T(2,128)} %bitcast.7), calls=%async_computation.3 | async-start | bytes 65536 | tf_op jit(solution)/shard_map/all_to_all | solution.py:28
  46.4 6.5 %convolution_bitcast_fusion = f32[1,32,2,8,128]{4,3,2,0,1:T(8,128)} fusion(bf16[32,2,512,128]{3,2,1,0:T(8,128)(2,1)} %param.7, f32[32,2,8,512]{3,2,1,0:T(8,128)S(1)} %get-tuple-element.6, f32[32,2,8]{2,1,0:T(2,128)} %get-tuple-element.5, pred[32,512]{1,0:T(8,128)(4,1)S(1)} %broadcast_compare_fusion), kind=kOutput, calls=%fused_computation.5 | convolution fusion | flops 403177472 | bytes 9717760 | tf_op jit(solution)/shard_map/bkgt,bktd->bkgd/dot_general | solution.py:23
  53.0 0.8 all-to-all-done.3
  53.8 6.7 %all-to-all-start.1 = ((f32[1,32,2,8,128]{4,3,2,0,1:T(8,128)}), f32[1,32,2,8,128]{4,3,2,0,1:T(8,128)S(1)}, u32[]{:S(2)}, u32[]{:S(2)}) async-start(f32[1,32,2,8,128]{4,3,2,0,1:T(8,128)} %convolution_bitcast_fusion), calls=%async_computation.1 | async-start | bytes 524288 | tf_op jit(solution)/shard_map/all_to_all | solution.py:29
  60.5 0.0 reduce-scatter.4.cloned.1.call-start
  60.5 0.1 fusion.15
  60.6 8.7 %all-to-all-done.1 = f32[1,32,2,8,128]{4,3,2,0,1:T(8,128)S(1)} async-done(((f32[1,32,2,8,128]{4,3,2,0,1:T(8,128)}), f32[1,32,2,8,128]{4,3,2,0,1:T(8,128)S(1)}, u32[]{:S(2)}, u32[]{:S(2)}) %all-to-all-start.1) | async-done | bytes 262176 | tf_op jit(solution)/shard_map/all_to_all | solution.py:29
  69.4 0.1 fusion.10
  69.5 0.1 fusion.17
  69.6 13.4 %fusion.2 = f32[5120,1]{1,0:T(8,128)} fusion(bf16[2,8,128,5120]{3,2,1,0:T(8,128)(2,1)} %param.9, bf16[2,8,128,1]{2,1,0,3:T(8,128)(2,1)S(1)} %fusion.17), kind=kOutput, calls=%fused_computation.2 | convolution fusion | flops 20971520 | bytes 20996096 | tf_op jit(solution)/shard_map/bkgd,kgdm->bm/dot_general | solution.py:36
  83.0 0.0 reduce-scatter.4.cloned.1.call-update
  83.0 31.6 %reduce-scatter.4.cloned.1.call-done = f32[1280,1]{1,0:T(8,128)} async-done(((f32[5120,1]{1,0:T(8,128)}), f32[1280,1]{1,0:T(8,128)}) %reduce-scatter.4.cloned.1.call-update) | async-done | bytes 5136
  114.7 1.9 %copy.11 = bf16[1,1280]{1,0:T(2,128)(2,1)} copy(f32[1,1280]{0,1:T(8,128)} %bitcast.46) | data formatting | bytes 7680
  (3 shorter events, 0.1 us)
Async XLA Ops:
  7.9 17.0 %all-to-all-start = ((bf16[32,1,2,8,128]{4,3,2,1,0:T(8,128)(2,1)}), bf16[32,1,2,8,128]{4,3,2,1,0:T(8,128)(2,1)S(1)}, u32[]{:S(2)}, u32[]{:S(2)}) async-start(bf16[32,1,2,8,128]{4,3,2,1,0:T(8,128)(2,1)} %stack.2), calls=%async_computation | async-start | bytes 262144 | tf_op jit(solution)/shard_map/all_to_all | solution.py:12
  31.3 11.3 %all-to-all-start.2 = ((f32[1,32,2,8]{3,2,0,1:T(2,128)}), f32[1,32,2,8]{3,2,0,1:T(2,128)S(1)}, u32[]{:S(2)}, u32[]{:S(2)}) async-start(f32[1,32,2,8]{3,2,0,1:T(2,128)} %bitcast.5), calls=%async_computation.2 | async-start | bytes 65536 | tf_op jit(solution)/shard_map/all_to_all | solution.py:27
  42.5 11.3 %all-to-all-start.3 = ((f32[1,32,2,8]{3,2,0,1:T(2,128)}), f32[1,32,2,8]{3,2,0,1:T(2,128)S(1)}, u32[]{:S(2)}, u32[]{:S(2)}) async-start(f32[1,32,2,8]{3,2,0,1:T(2,128)} %bitcast.7), calls=%async_computation.3 | async-start | bytes 65536 | tf_op jit(solution)/shard_map/all_to_all | solution.py:28
  53.8 15.6 %all-to-all-start.1 = ((f32[1,32,2,8,128]{4,3,2,0,1:T(8,128)}), f32[1,32,2,8,128]{4,3,2,0,1:T(8,128)S(1)}, u32[]{:S(2)}, u32[]{:S(2)}) async-start(f32[1,32,2,8,128]{4,3,2,0,1:T(8,128)} %convolution_bitcast_fusion), calls=%async_computation.1 | async-start | bytes 524288 | tf_op jit(solution)/shard_map/all_to_all | solution.py:29
  60.5 54.2 %reduce-scatter.4.cloned.1.call-start = ((), (), s32[]{:S(2)}) async-start(), calls=%async_computation.5 | async-start | bytes 3276800
Sparse Core Ops, SparseCore 0:
  83.2 31.4 reduce-scatter.3
